TPU v7x, 256 devices: a whole 4x4x8 slice. The times are simulated.
256 devices in a mesh: depth: 2 (over y_hi), row: 16 (over z, y_lo), col: 8 (over x, core).
Axes of the slice: x: 4, y: 4 (y_hi: 2, y_lo: 2; y = y_hi * 2 + y_lo), z: 8, core: 2. Of those that a mesh axis runs over, the one named last changes fastest.
Arguments:
- features: bfloat16 [128, 576, 1152], P('row', 'col', 'depth'), may hold values from -6 to 6
- w_in: bfloat16 [1152, 4096], P('depth'), may hold values from -0.1875 to 0.1875
- b_in: float32 [4096], replicated, may hold values from -4 to 4
- w_out: bfloat16 [4096, 4096], P('row', 'depth'), may hold values from -0.09375 to 0.09375
- b_out: float32 [4096], P('depth'), may hold values from -3 to 3
- text: bfloat16 [128, 448, 4096], P(('row', 'col'), None, 'depth'), may hold values from -6 to 6
- offsets: int32 [128], P(('row', 'col')), may hold values from 0 to 448
Outputs:
- sequences: bfloat16 [128, 1024, 4096], P(('row', 'col'), None, 'depth')
Inputs may be any that keep to these rules, and one draw needn't show every extreme that they name: offsets[i] is where image i's first patch stands in sequence i.
All inputs are finite; a program needn't handle non-finite values.
Results may differ from a plain program's by a relative error of at most 0.007.
Values may be sent and summed in bfloat16 or wider, within the bound.
A program may use at most 128 MiB of HBM per device.

v0:
```python
import jax
import jax.numpy as jnp
from jax import lax
from jax.sharding import PartitionSpec as P


def cut_along(x, dim, length):
    shape = x.shape
    parts = x.reshape(*shape[:dim], length, shape[dim] // length, *shape[dim + 1 :])
    return jnp.moveaxis(parts, dim, 0)


def summed_on_arrival(x, axis, dim):
    length = lax.axis_size(axis)
    parts = lax.all_to_all(cut_along(x, dim, length), axis, 0, 0, tiled=True)
    return jnp.sum(parts.astype(jnp.float32), axis=0)


def sent_to_all(x, axis):
    length = lax.axis_size(axis)
    return lax.all_to_all(jnp.broadcast_to(x[None], (length, *x.shape)), axis, 0, 0, tiled=True)


def joined_along(parts, dim):
    shape = list(parts.shape[1:])
    shape[dim] *= parts.shape[0]
    return jnp.moveaxis(parts, 0, dim).reshape(shape)


def collect(x, axis, dim):
    parts = sent_to_all(x, axis)
    return joined_along(parts, dim)


def place_image(image_rows, text_rows, offset):
    patch_count = image_rows.shape[0]
    text_count = text_rows.shape[0]
    width = image_rows.shape[1]
    length = patch_count + text_count
    positions = jnp.arange(length, dtype=jnp.int32)
    zeros_text = jnp.zeros((text_count, width), image_rows.dtype)
    padded = jnp.concatenate([zeros_text, image_rows, zeros_text], 0)
    shifted = lax.dynamic_slice_in_dim(padded, text_count - offset, length, 0)
    zeros_patch = jnp.zeros((patch_count, width), text_rows.dtype)
    early = jnp.concatenate([text_rows, zeros_patch], 0)
    later = jnp.concatenate([zeros_patch, text_rows], 0)
    inside = (positions >= offset) & (positions < offset + patch_count)
    before = positions < offset
    return jnp.where(inside[:, None], shifted, jnp.where(before[:, None], early, later))


def on_device(features, w_in, b_in, w_out, b_out, text, offsets):
    image_count, patch_count, half_width = features.shape
    token_rows = features.reshape(image_count * patch_count, half_width)
    partial_pre = jnp.dot(token_rows, w_in, preferred_element_type=jnp.float32)
    share_pre = summed_on_arrival(partial_pre.astype(jnp.bfloat16), "depth", 0)
    hidden_share = jax.nn.gelu(share_pre + b_in, approximate=False).astype(jnp.bfloat16)
    hidden = collect(hidden_share, "depth", 0)
    out_width = w_out.shape[1]
    part_rows = w_out.shape[0] // lax.axis_size("col")
    start_row = lax.axis_index("col") * part_rows
    own_part = lax.dynamic_slice_in_dim(w_out, start_row, part_rows, 0)
    out_sum = jnp.dot(
        hidden,
        lax.all_gather(own_part, ("row", "col"), axis=0, tiled=True),
        preferred_element_type=jnp.float32,
    )
    projected = (out_sum + b_out).astype(jnp.bfloat16).reshape(image_count, patch_count, out_width)
    arranged = lax.all_to_all(projected, "col", split_axis=0, concat_axis=1, tiled=True)
    return jax.vmap(place_image)(arranged, text, offsets)


def solution(mesh):
    return jax.shard_map(
        on_device,
        mesh=mesh,
        in_specs=(
            P("row", "col", "depth"),
            P("depth", None),
            P(),
            P("row", "depth"),
            P("depth"),
            P(("row", "col"), None, "depth"),
            P(("row", "col")),
        ),
        out_specs=P(("row", "col"), None, "depth"),
        check_vma=False,
    )
```

profile of v0, /device:TPU:1, one launch (start us, length us, event | category | flops | bytes accessed | tf_op | source)
XLA Modules:
  0.0 311.2 jit_solution(4737258590934388490)
XLA Ops:
  6.5 0.0 copy-start
  6.5 0.0 all-gather.2.cloned.1.call-start
  6.5 1.2 copy-done
  7.8 0.7 constant_dynamic-slice_fusion
  8.4 0.0 all-gather.2.cloned.1.call-update
  8.4 6.4 %convolution_convert_fusion = bf16[576,4096]{1,0:T(8,128)(2,1)S(1)} fusion(bf16[576,576]{1,0:T(8,128)(2,1)} %bitcast.17, bf16[576,4096]{1,0:T(8,128)(2,1)} %param.8), kind=kOutput, calls=%fused_computation.2 | convolution fusion | flops 2720268288 | bytes 10100736 | tf_op jit(solution)/shard_map/dot_general | solution.py:55
  14.9 58.1 %all_to_all.22 = bf16[2,288,4096]{2,1,0:T(8,128)(2,1)S(1)} all-to-all(bf16[2,288,4096]{2,1,0:T(8,128)(2,1)S(1)} %bitcast.15), channel_id=1, replica_groups=mesh['depth'=2,'row'=16,'col'=8] {'depth'}, dimensions={0} | all-to-all | bytes 9437184 | tf_op jit(solution)/shard_map/all_to_all | solution.py:15
  73.0 0.0 copy-start.1
  73.0 1.1 convert_reduce_fusion
  74.1 0.0 copy-done.1
  74.1 10.3 %fusion.2 = bf16[288,4096]{1,0:T(8,128)(2,1)S(1)} fusion(f32[288,4096]{1,0:T(8,128)S(1)} %convert_reduce_fusion, f32[4096]{0:T(1024)S(1)} %copy-done.1), kind=kLoop, calls=%fused_computation.8 | loop fusion | flops 77856768 | bytes 7094272 | tf_op jit(solution)/shard_map/convert_element_type | solution.py:57
  84.4 0.6 broadcast_in_dim.15
  85.0 0.0 copy-start.2
  85.0 56.3 %all_to_all.23 = bf16[2,288,4096]{2,1,0:T(8,128)(2,1)} all-to-all(bf16[2,288,4096]{2,1,0:T(8,128)(2,1)S(1)} %broadcast_in_dim.15), channel_id=1, replica_groups=mesh['depth'=2,'row'=16,'col'=8] {'depth'}, dimensions={0} | all-to-all | bytes 9437184 | tf_op jit(solution)/shard_map/all_to_all | solution.py:21
  141.3 98.5 %all-gather.2.cloned.1.call-done = bf16[4096,2048]{1,0:T(8,128)(2,1)} async-done(((bf16[32,2048]{1,0:T(8,128)(2,1)}), bf16[4096,2048]{1,0:T(8,128)(2,1)}) %all-gather.2.cloned.1.call-update) | async-done | bytes 16777232 | tf_op jit(solution)/shard_map/all_gather | solution.py:65
  239.8 0.0 copy-done.2
  239.8 15.8 %add_convert_fusion = bf16[576,2048]{1,0:T(8,128)(2,1)} fusion(bf16[576,4096]{1,0:T(8,128)(2,1)} %bitcast.14, bf16[4096,2048]{1,0:T(8,128)(2,1)} %all-gather.2.cloned.1.call-done, f32[2048]{0:T(1024)S(1)} %copy-done.2), kind=kOutput, calls=%fused_computation.9 | convolution fusion | flops 9666035712 | bytes 23863296 | tf_op jit(solution)/shard_map/dot_general | solution.py:63
  255.6 4.6 %all-to-all-start.2 = ((bf16[8,72,2048]{2,1,0:T(8,128)(2,1)}), bf16[8,72,2048]{2,1,0:T(8,128)(2,1)S(1)}, u32[]{:S(2)}, u32[]{:S(2)}) async-start(bf16[8,72,2048]{2,1,0:T(8,128)(2,1)} %bitcast.16), calls=%async_computation.2 | async-start | bytes 4718592 | tf_op jit(solution)/shard_map/all_to_all | solution.py:69
  260.9 28.4 %all-to-all-done.2 = bf16[8,72,2048]{2,1,0:T(8,128)(2,1)S(1)} async-done(((bf16[8,72,2048]{2,1,0:T(8,128)(2,1)}), bf16[8,72,2048]{2,1,0:T(8,128)(2,1)S(1)}, u32[]{:S(2)}, u32[]{:S(2)}) %all-to-all-start.2) | async-done | bytes 2359328 | tf_op jit(solution)/shard_map/all_to_all | solution.py:69
  289.3 0.2 broadcast.186
  289.5 14.9 %fusion.12 = bf16[1,1024,2048]{2,1,0:T(8,128)(2,1)} fusion(s32[]{:T(128)} %bitcast.7, bf16[1,448,2048]{2,1,0:T(8,128)(2,1)S(1)} %broadcast.186, bf16[1,576,2048]{2,1,0:T(8,128)(2,1)S(1)} %bitcast.13, bf16[1,448,2048]{2,1,0:T(8,128)(2,1)} %param.12, pred[1024]{0:T(1024)(128)(4,1)S(1)} %get-tuple-element.16, pred[1024]{0:T(1024)(128)(4,1)S(1)} %get-tuple-element.17), kind=kLoop, calls=%fused_computation.27 | loop fusion | flops 16777216 | bytes 10225668 | tf_op jit(solution)/shard_map/vmap(jit(_where))/select_n | solution.py:49
  (1 shorter events, 0.0 us)
Async XLA Ops:
  6.5 1.2 copy-start
  6.5 233.3 %all-gather.2.cloned.1.call-start = ((), (), s32[]{:S(2)}) async-start(), calls=%async_computation.3 | async-start | bytes 16908288 | tf_op jit(solution)/shard_map/all_gather | solution.py:65
  73.0 1.1 copy-start.1
  85.0 154.8 %copy-start.2 = (f32[2048]{0:T(1024)S(1)}, f32[2048]{0:T(1024)}, u32[]{:S(2)}) copy-start(f32[2048]{0:T(1024)} %param.11) | copy-start | bytes 24580
  255.6 33.7 %all-to-all-start.2 = ((bf16[8,72,2048]{2,1,0:T(8,128)(2,1)}), bf16[8,72,2048]{2,1,0:T(8,128)(2,1)S(1)}, u32[]{:S(2)}, u32[]{:S(2)}) async-start(bf16[8,72,2048]{2,1,0:T(8,128)(2,1)} %bitcast.16), calls=%async_computation.2 | async-start | bytes 4718592 | tf_op jit(solution)/shard_map/all_to_all | solution.py:69
Sparse Core Ops, SparseCore 0:
  9.2 230.5 all-gather.1
where the time goes:
time: 312 us; the launch traced here: 311 us
  waiting for transfers between devices  127 us (41%)
  blocking collectives  114 us (37%)
  other arithmetic  26.2 us (8%)
  matrix products  22.2 us (7%)
  between operations  14.1 us (5%)
  starting transfers between devices  4.63 us (1%)
    all_gather x1, waiting for transfers between devices, on_device(): lax.all_gather(own_part, ('row', 'col'), axis=0, tiled=True)  98.5 us
    all_to_all x1, blocking collectives, summed_on_arrival(): parts = lax.all_to_all(cut_along(x, dim, length), axis, 0, 0, tiled=True)  58.1 us
    all_to_all x1, blocking collectives, sent_to_all(): lax.all_to_all(jnp.broadcast_to(x[None], (length, *x.shape)), axis, 0, 0,...  56.3 us
    all_to_all x1, waiting for transfers between devices, on_device(): lax.all_to_all(projected, 'col', split_axis=0, concat_axis=1, tiled=True)  28.4 us
    dot_general x1, matrix products, on_device(): jnp.dot(hidden, lax.all_gather(own_part, ('row', 'col'), axis=0, tiled=Tr...  15.8 us
    select_n x1, other arithmetic, place_image(): jnp.where(inside[:, None], shifted, jnp.where(before[:, None], early, lat...  14.9 us
    convert_element_type x1, other arithmetic, on_device(): jax.nn.gelu(share_pre + b_in, approximate=False).astype(jnp.bfloat16)  10.3 us
    dot_general x1, matrix products, on_device(): partial_pre = jnp.dot(token_rows, w_in, preferred_element_type=jnp.float32)  6.4 us
  transfers between devices with their start and end apart: 2, of which 2 were waited for; matrix products, arithmetic and copies ran while one was open for 6% of the time, Pallas kernels for 0%

commit v1 on v0

v1 whole, which is shorter than its diff:
```python
import functools

import jax
import jax.numpy as jnp
from jax import lax
from jax.experimental import pallas as pl
from jax.experimental.pallas import tpu as pltpu
from jax.sharding import PartitionSpec as P

TILE = 16


def place_kernel(offset_ref, image_ref, text_ref, out_ref):
    offset = offset_ref[0]
    text_count = text_ref.shape[0]
    padded = image_ref.shape[0]
    patch_count = padded - TILE
    shift = lax.rem(offset, TILE)
    base = pl.multiple_of(offset - shift, TILE)
    out_ref[:text_count, :] = text_ref[...]
    out_ref[patch_count:, :] = text_ref[...]
    out_ref[pl.ds(pl.multiple_of(base + TILE, TILE), patch_count - TILE), :] = image_ref[TILE:patch_count, :]
    edge = pl.multiple_of(jnp.minimum(base, text_count - TILE), TILE)
    beside = text_ref[pl.ds(edge, TILE), :]
    rows = lax.broadcasted_iota(jnp.int32, beside.shape, 0)
    out_ref[pl.ds(base, TILE), :] = jnp.where(rows >= shift, image_ref[:TILE, :], beside)

    @pl.when(base < text_count)
    def _():
        below = jnp.where(rows < shift, image_ref[patch_count:, :], beside)
        out_ref[pl.ds(pl.multiple_of(base + patch_count, TILE), TILE), :] = below


def place(image_rows, text_rows, offset, width=512):
    padded, columns = image_rows.shape
    text_count = text_rows.shape[0]
    length = padded - TILE + text_count
    return pl.pallas_call(
        place_kernel,
        out_shape=jax.ShapeDtypeStruct((length, columns), image_rows.dtype),
        grid_spec=pltpu.PrefetchScalarGridSpec(
            num_scalar_prefetch=1,
            grid=(columns // width,),
            in_specs=[
                pl.BlockSpec((padded, width), lambda i, o: (0, i)),
                pl.BlockSpec((text_count, width), lambda i, o: (0, i)),
            ],
            out_specs=pl.BlockSpec((length, width), lambda i, o: (0, i)),
        ),
        name="place",
    )(offset, image_rows, text_rows)


def on_device(features, w_in, b_in, w_out, b_out, text, offsets):
    col = lax.axis_index("col")
    cols = lax.axis_size("col")
    image = lax.all_to_all(features, "col", split_axis=0, concat_axis=1, tiled=True)[0]
    image = lax.all_gather(image, "depth", axis=1, tiled=True)
    patch_count = image.shape[0]
    shift = lax.rem(offsets[0], TILE)
    spots = jnp.arange(patch_count + TILE, dtype=jnp.int32)[:, None] - shift
    moved = (spots == jnp.arange(patch_count, dtype=jnp.int32)[None, :]).astype(jnp.bfloat16)
    image = jnp.dot(moved, image, preferred_element_type=jnp.float32).astype(jnp.bfloat16)

    part = w_in.shape[0] // cols
    own_in = lax.dynamic_slice_in_dim(w_in, col * part, part, 0)
    full_in = lax.all_gather(own_in, ("depth", "col"), axis=0, tiled=True)
    pre = jnp.dot(image, full_in, preferred_element_type=jnp.float32) + b_in
    hidden = jax.nn.gelu(pre, approximate=False).astype(jnp.bfloat16)

    part = w_out.shape[0] // cols
    own_out = lax.dynamic_slice_in_dim(w_out, col * part, part, 0)
    full_out = lax.all_gather(own_out, ("row", "col"), axis=0, tiled=True)
    total = jnp.dot(hidden, full_out, preferred_element_type=jnp.float32)
    projected = (total + b_out).astype(jnp.bfloat16)
    return place(projected, text[0], offsets)[None]


def solution(mesh):
    return jax.shard_map(
        on_device,
        mesh=mesh,
        in_specs=(
            P("row", "col", "depth"),
            P("depth", None),
            P(),
            P("row", "depth"),
            P("depth"),
            P(("row", "col"), None, "depth"),
            P(("row", "col")),
        ),
        out_specs=P(("row", "col"), None, "depth"),
        check_vma=False,
    )
```

time: 312 us -> 400 us (1.28)
  waiting for transfers between devices: 127 us -> 310 us
  blocking collectives: 114 us -> 18.4 us
  matrix products: 22.2 us -> 48.4 us
  other arithmetic: 26.2 us -> 0.01 us
  Pallas kernels: 0 us -> 4.75 us
  starting transfers between devices: 4.63 us -> 0.09 us
    all_gather x1 -> x3, waiting for transfers between devices: 98.5 us -> 310 us  [the longest x1 198 us: on_device(): full_out = lax.all_gather(own_out, ('row', 'col'), axis=0, tiled=True)]
    all_to_all x2 -> x1, blocking collectives: 114 us -> 18.4 us  [on_device(): lax.all_to_all(features, 'col', split_axis=0, concat_axis=1, tiled=True)[0]]
    all_to_all x1 -> x0, waiting for transfers between devices: 28.4 us -> none  [on_device(): lax.all_to_all(projected, 'col', split_axis=0, concat_axis=1, tiled=True)]
    dot_general x2 -> x3, matrix products: 22.2 us -> 48.4 us  [the longest x1 29.5 us: on_device(): pre = jnp.dot(image, full_in, preferred_element_type=jnp.float32) + b_in]
    select_n x1 -> x0, other arithmetic: 14.9 us -> none  [place_image(): jnp.where(inside[:, None], shifted, jnp.where(before[:, None], early, lat...]
    convert_element_type x1 -> x0, other arithmetic: 10.3 us -> none  [on_device(): jax.nn.gelu(share_pre + b_in, approximate=False).astype(jnp.bfloat16)]
    pallas_call x0 -> x1, Pallas kernels: none -> 4.75 us  [place(): pl.pallas_call(place_kernel, out_shape=jax.ShapeDtypeStruct((length, colu...]
    all_to_all x1 -> x0, starting transfers between devices: 4.63 us -> none  [on_device(): lax.all_to_all(projected, 'col', split_axis=0, concat_axis=1, tiled=True)]
  transfers between devices with their start and end apart: 2 -> 3, of which waited for: 2 -> 3; matrix products, arithmetic and copies ran while one was open for 6% -> 9% of each run, Pallas kernels for 0% -> 0%
where the time goes in v1:
time: 400 us; the launch traced here: 399 us
  waiting for transfers between devices  310 us (78%)
  matrix products  48.4 us (12%)
  blocking collectives  18.4 us (5%)
  between operations  13.8 us (3%)
  Pallas kernels  4.75 us (1%)
    all_gather x1, waiting for transfers between devices, on_device(): full_out = lax.all_gather(own_out, ('row', 'col'), axis=0, tiled=True)  198 us
    all_gather x1, waiting for transfers between devices, on_device(): full_in = lax.all_gather(own_in, ('depth', 'col'), axis=0, tiled=True)  82 us
    all_gather x1, waiting for transfers between devices, on_device(): image = lax.all_gather(image, 'depth', axis=1, tiled=True)  29.8 us
    dot_general x1, matrix products, on_device(): pre = jnp.dot(image, full_in, preferred_element_type=jnp.float32) + b_in  29.5 us
    all_to_all x1, blocking collectives, on_device(): lax.all_to_all(features, 'col', split_axis=0, concat_axis=1, tiled=True)[0]  18.4 us
    dot_general x1, matrix products, on_device(): total = jnp.dot(hidden, full_out, preferred_element_type=jnp.float32)  16.1 us
  transfers between devices with their start and end apart: 3, of which 3 were waited for; matrix products, arithmetic and copies ran while one was open for 9% of the time, Pallas kernels for 0%

profile of v1, /device:TPU:1, one launch (start us, length us, event | category | flops | bytes accessed | tf_op | source)
XLA Modules:
  0.0 399.3 jit_solution(7601124040145222089)
XLA Ops:
  6.5 0.0 copy-start
  6.5 0.0 copy-start.1
  6.5 0.0 all-gather.4.cloned.1.call-start
  6.5 18.4 %all_to_all.4 = bf16[8,72,576]{2,1,0:T(8,128)(2,1)S(1)} all-to-all(bf16[8,72,576]{2,1,0:T(8,128)(2,1)} %param.7), channel_id=1, replica_groups=mesh['depth'=2,'row'=16,'col'=8] {'col'}, dimensions={0} | all-to-all | bytes 1327104 | tf_op jit(solution)/shard_map/all_to_all | solution.py:57
  25.0 1.2 copy.9
  26.2 0.0 all-gather.4.cloned.1.call-update
  26.2 0.0 all-gather.6.cloned.1.call-start
  26.2 1.9 constant_dynamic-slice_fusion.1
  28.2 0.0 all-gather.6.cloned.1.call-update
  28.2 0.0 all-gather.8.cloned.1.call-start
  28.2 0.0 copy-done
  28.2 0.7 constant_dynamic-slice_fusion
  28.9 0.0 all-gather.8.cloned.1.call-update
  29.6 29.8 %all-gather.4.cloned.1.call-done = bf16[576,1152]{0,1:T(8,128)(2,1)} async-done(((bf16[576,576]{0,1:T(8,128)(2,1)}), bf16[576,1152]{0,1:T(8,128)(2,1)}) %all-gather.4.cloned.1.call-update) | async-done | bytes 1327120 | tf_op jit(solution)/shard_map/all_gather | solution.py:58
  59.4 2.8 convolution_convert_fusion
  62.2 0.0 copy-start.2
  62.2 82.0 %all-gather.6.cloned.1.call-done = bf16[1152,4096]{1,0:T(8,128)(2,1)} async-done(((bf16[72,4096]{1,0:T(8,128)(2,1)}), bf16[1152,4096]{1,0:T(8,128)(2,1)}) %all-gather.6.cloned.1.call-update) | async-done | bytes 9437200 | tf_op jit(solution)/shard_map/all_gather | solution.py:67
  144.3 0.0 copy-done.1
  144.3 29.5 %fusion.2.clone.6 = bf16[592,4096]{1,0:T(8,128)(2,1)} fusion(bf16[592,1152]{1,0:T(8,128)(2,1)S(1)} %convolution_convert_fusion, bf16[1152,4096]{1,0:T(8,128)(2,1)} %all-gather.6.cloned.1.call-done, f32[4096]{0:T(1024)S(1)} %copy-done.1), kind=kOutput, calls=%fused_computation.3.clone.clone.clone.clone.clone.1 | convolution fusion | flops 5746851840 | bytes 15667200 | tf_op jit(solution)/shard_map/dot_general | solution.py:68
  173.8 198.1 %all-gather.8.cloned.1.call-done = bf16[4096,2048]{1,0:T(8,128)(2,1)} async-done(((bf16[32,2048]{1,0:T(8,128)(2,1)}), bf16[4096,2048]{1,0:T(8,128)(2,1)}) %all-gather.8.cloned.1.call-update) | async-done | bytes 16777232 | tf_op jit(solution)/shard_map/all_gather | solution.py:73
  371.9 0.0 copy-done.2
  371.9 16.1 %add_convert_fusion.image_ref = bf16[592,2048]{1,0:T(8,128)(2,1)} fusion(bf16[4096,2048]{1,0:T(8,128)(2,1)} %all-gather.8.cloned.1.call-done, f32[2048]{0:T(1024)S(1)} %copy-done.2, bf16[592,4096]{1,0:T(8,128)(2,1)} %fusion.2.clone.6), kind=kOutput, calls=%fused_computation.20 | convolution fusion | flops 9934536704 | bytes 24059904 | tf_op jit(solution)/shard_map/dot_general | solution.py:74
  388.0 4.8 %place.1 = bf16[1024,2048]{1,0:T(8,128)(2,1)} custom-call(s32[1]{0:T(128)} %copy.10.offset_ref, bf16[592,2048]{1,0:T(8,128)(2,1)} %add_convert_fusion.image_ref, bf16[448,2048]{1,0:T(8,128)(2,1)} %bitcast.20), custom_call_target="tpu_custom_call" | custom-call | tf_op jit(solution)/shard_map/place/pallas_call | solution.py:38
  (1 shorter events, 0.0 us)
Async XLA Ops:
  6.5 21.7 %copy-start = (bf16[256,2048]{1,0:T(8,128)(2,1)S(1)}, bf16[256,2048]{1,0:T(8,128)(2,1)}, u32[]{:S(2)}) copy-start(bf16[256,2048]{1,0:T(8,128)(2,1)} %param.10) | copy-start | bytes 3145732
  6.5 137.7 %copy-start.1 = (f32[4096]{0:T(1024)S(1)}, f32[4096]{0:T(1024)}, u32[]{:S(2)}) copy-start(f32[4096]{0:T(1024)} %param.9) | copy-start | bytes 49156
  6.5 52.9 %all-gather.4.cloned.1.call-start = ((), (), s32[]{:S(2)}) async-start(), calls=%async_computation.1 | async-start | bytes 2211840 | tf_op jit(solution)/shard_map/all_gather | solution.py:58
  26.2 118.1 %all-gather.6.cloned.1.call-start = ((), (), s32[]{:S(2)}) async-start(), calls=%async_computation.2 | async-start | bytes 10027008 | tf_op jit(solution)/shard_map/all_gather | solution.py:67
  28.2 343.7 %all-gather.8.cloned.1.call-start = ((), (), s32[]{:S(2)}) async-start(), calls=%async_computation.3 | async-start | bytes 16908288 | tf_op jit(solution)/shard_map/all_gather | solution.py:73
  62.2 309.7 %copy-start.2 = (f32[2048]{0:T(1024)S(1)}, f32[2048]{0:T(1024)}, u32[]{:S(2)}) copy-start(f32[2048]{0:T(1024)} %param.11) | copy-start | bytes 24580
Sparse Core Ops, SparseCore 0:
  26.3 33.0 all-gather.3
  62.1 82.0 all-gather.5
  146.1 225.7 all-gather.7

commit v2 on v1

--- a/solution.py
+++ b/solution.py
@@ -8,6 +8,10 @@
 from jax.sharding import PartitionSpec as P
 
 TILE = 16
+MESH = pl.DeviceIdType.MESH
+STEPS = 8
+SLABS = 8
+GROUP = 128
 
 
 def place_kernel(offset_ref, image_ref, text_ref, out_ref):
@@ -51,28 +55,420 @@
     )(offset, image_rows, text_rows)
 
 
+def project_kernel(
+    shift_ref, features, w_in, b_in, w_out, b_out, out_ref,
+    own_slabs, relay_slabs, far_slabs, tokens, own_image, far_image,
+    own_in, far_in, pre, hidden, weights, total,
+    local_sem, send_sem, recv_sem,
+):
+    depth, row, col = lax.axis_index("depth"), lax.axis_index("row"), lax.axis_index("col")
+    z, low = lax.div(row, 2), lax.rem(row, 2)
+    x, core = lax.div(col, 2), lax.rem(col, 2)
+    twin = 2 * z + 1 - low
+    beside = (depth, twin, col)
+    across = (1 - depth, twin, col)
+    up = (depth, 2 * lax.rem(z + 1, 8) + low, col)
+    down = (depth, 2 * lax.rem(z + 7, 8) + low, col)
+    ahead = (depth, row, 2 * lax.rem(x + 1, 4) + core)
+    behind = (depth, row, 2 * lax.rem(x + 3, 4) + core)
+    mate = (depth, row, 2 * x + 1 - core)
+
+    def column(step, flip):
+        return 2 * lax.rem(x + step, 4) + (1 - core if flip else core)
+
+    def z_of(j):
+        half, odd = lax.div(j + 1, 2), lax.rem(j, 2)
+        return lax.rem(z + 8 + half * (1 - 2 * odd), 8)
+
+    count = [0, 0]
+    sent = []
+
+    def local(source, target):
+        copy = pltpu.make_async_copy(source, target, local_sem.at[count[0]])
+        count[0] += 1
+        copy.start()
+        return copy
+
+    def send(source, target, device):
+        n = count[1]
+        count[1] += 1
+        copy = pltpu.make_async_remote_copy(
+            src_ref=source, dst_ref=target, send_sem=send_sem.at[n], recv_sem=recv_sem.at[n],
+            device_id=device, device_id_type=MESH,
+        )
+        copy.start()
+        sent.append(copy)
+        return copy
+
+    def group_column(half, group):
+        if group < 4:
+            return 1024 * half + GROUP * group
+        return 1024 * half + 512 + GROUP * lax.rem(x + group - 4, 4)
+
+    own_weights = {}
+    for near in (True, False):
+        for group in range(8):
+            half = core if near else 1 - core
+            start = pl.multiple_of(group_column(half, group), GROUP)
+            own_weights[near, group] = local(w_out.at[:, pl.ds(start, GROUP)], weights.at[row, half, group])
+    own_slab = local(features.at[col], own_slabs.at[col])
+    in_copies = []
+    for j in range(STEPS):
+        start = pl.multiple_of(512 * z_of(j), 512)
+        in_copies.append(local(w_in.at[:, :, pl.ds(start, 512)], own_in.at[j]))
+
+    others = [(0, True), (1, False), (1, True), (3, False), (3, True), (2, False), (2, True)]
+    partners = [(depth, row, column(*other)) for other in others] + [beside, across, up, down]
+    barrier = pltpu.get_barrier_semaphore()
+    for partner in partners:
+        pl.semaphore_signal(barrier, inc=1, device_id=partner, device_id_type=MESH)
+    pl.semaphore_wait(barrier, len(partners))
+
+    ring_up, ring_down, unit_mate, quarter, opposite, rest_mate = {}, {}, {}, {}, {}, {}
+
+    def unit(b):
+        return weights.at[b, core, pl.ds(0, 5)]
+
+    def arrived_from(t, s, sign):
+        return 2 * lax.rem(z + 8 + sign * t, 8) + (low if s == 0 else 1 - low)
+
+    def onward(b, t, s, sign):
+        ring = ring_up if sign < 0 else ring_down
+        if t < 3 or (t == 3 and s == (0 if sign < 0 else 1)):
+            ring[t, s] = send(unit(b), unit(b), up if sign < 0 else down)
+
+    def spread(b, key):
+        quarter[key] = (
+            send(weights.at[b, core, 4], weights.at[b, core, 7], ahead),
+            send(weights.at[b, core, 4], weights.at[b, core, 5], behind),
+        )
+        unit_mate[key] = send(unit(b), unit(b), mate)
+
+    def block_of(key):
+        t, s, sign = key
+        return arrived_from(t, s, sign)
+
+    def units(keys):
+        for key in keys:
+            t, s, sign = key
+            (ring_up if sign < 0 else ring_down)[t - 1, s].wait_recv()
+            onward(block_of(key), t, s, sign)
+        for key in keys:
+            spread(block_of(key), key)
+
+    def quarters(keys):
+        for key in keys:
+            b = block_of(key)
+            for copy in quarter[key]:
+                copy.wait_recv()
+            first, second = pl.ds(0, 128), pl.ds(128, 128)
+            opposite[key] = (
+                send(weights.at[b, core, 7, first], weights.at[b, core, 6, first], ahead),
+                send(weights.at[b, core, 5, second], weights.at[b, core, 6, second], behind),
+            )
+
+    def opposites(keys):
+        for key in keys:
+            b = block_of(key)
+            for copy in opposite[key]:
+                copy.wait_recv()
+            rest_mate[key] = send(weights.at[b, core, pl.ds(5, 3)], weights.at[b, core, pl.ds(5, 3)], mate)
+
+    def complete(keys):
+        for key in keys:
+            unit_mate[key].wait_recv()
+            rest_mate[key].wait_recv()
+
+    for group in range(5):
+        own_weights[True, group].wait()
+    onward(row, 0, 0, -1)
+    onward(row, 0, 0, 1)
+    twin_unit = send(unit(row), unit(row), beside)
+    slab_copies = {}
+    for other in [others[1], others[2], others[3], others[4], others[5], others[6], others[0]]:
+        target = column(*other)
+        slab_copies[other] = send(features.at[target], own_slabs.at[col], (depth, row, target))
+
+    mine, next_to = 2 * low + core, 2 * (1 - low) + core
+    in_across, in_beside, in_mate, in_mate_next = {}, {}, {}, {}
+
+    def in_start(j):
+        in_copies[j].wait()
+        in_across[j] = send(own_in.at[j, next_to], far_in.at[j, next_to], across)
+
+    def in_pass(j):
+        in_across[j].wait_recv()
+        in_beside[j] = send(far_in.at[j, mine], far_in.at[j, mine], beside)
+        in_mate[j] = send(far_in.at[j, mine], far_in.at[j, mine], mate)
+
+    def in_pass_next(j):
+        in_beside[j].wait_recv()
+        in_mate_next[j] = send(far_in.at[j, next_to], far_in.at[j, next_to], mate)
+
+    def in_complete(j):
+        in_mate[j].wait_recv()
+        in_mate_next[j].wait_recv()
+
+    in_start(0)
+    in_start(1)
+
+    hops, lasts, slab_at = [], [], []
+
+    def hop(slab):
+        n = len(hops)
+        slab_at.append(slab)
+        hops.append(send(own_slabs.at[slab], relay_slabs.at[slab], beside if n % 2 == 0 else across))
+
+    def relay(n):
+        hops[n].wait_recv()
+        slab = slab_at[n]
+        lasts.append(send(relay_slabs.at[slab], far_slabs.at[slab], across if n % 2 == 0 else beside))
+
+    def source_of(other):
+        step, flip = other
+        return column((4 - step) % 4, flip)
+
+    def take(other):
+        slab_copies[other].wait_recv()
+        hop(source_of(other))
+
+    own_slab.wait()
+    hop(col)
+    for other in (others[0], others[1], others[2], others[3], others[4]):
+        take(other)
+    relay(0)
+    relay(1)
+    twin_unit.wait_recv()
+    twin_key = (0, 1, 1)
+    onward(twin, 0, 1, -1)
+    onward(twin, 0, 1, 1)
+    spread(twin, twin_key)
+    take(others[5])
+    take(others[6])
+    for n in range(2, 6):
+        relay(n)
+
+    patch_count = tokens.shape[0]
+    spots = lax.broadcasted_iota(jnp.int32, (patch_count + TILE, patch_count), 0) - shift_ref[0]
+    moved = (spots == lax.broadcasted_iota(jnp.int32, spots.shape, 1)).astype(jnp.float32).astype(jnp.bfloat16)
+
+    def assemble(slabs, image):
+        height = slabs.shape[1]
+        for slab in range(SLABS):
+            tokens[slab * height : (slab + 1) * height, :] = slabs[slab].astype(jnp.float32)
+        image[...] = jnp.dot(
+            moved, tokens[...].astype(jnp.bfloat16), preferred_element_type=jnp.float32
+        ).astype(jnp.bfloat16)
+
+    def half_columns(n):
+        return pl.ds(pl.multiple_of(256 * n, 256), 256)
+
+    def own_layer(first, last):
+        def body(i, carry):
+            j, n = lax.div(i, 2), lax.rem(i, 2)
+            rhs = own_in[j, :, :, half_columns(n)].reshape(-1, 256)
+            pre[j, :, half_columns(n)] = jnp.dot(own_image[...], rhs, preferred_element_type=jnp.float32)
+            return carry
+
+        lax.fori_loop(2 * first, 2 * last, body, 0)
+
+    def first_layer(first, last):
+        def body(i, carry):
+            j, n = lax.div(i, 2), lax.rem(i, 2)
+            rhs = far_in[j, :, :, half_columns(n)].reshape(-1, 256)
+            value = pre[j, :, half_columns(n)] + jnp.dot(far_image[...], rhs, preferred_element_type=jnp.float32)
+            value = value + b_in[pl.ds(z_of(j), 1), half_columns(n)]
+            value = 0.5 * value * (1.0 + lax.erf(value * 0.7071067811865476))
+            hidden[j, :, half_columns(n)] = value.astype(jnp.bfloat16)
+            return carry
+
+        lax.fori_loop(2 * first, 2 * last, body, 0)
+
+    def product(j, n):
+        half, group = lax.div(n, 4), 2 * lax.rem(n, 4)
+        b = 2 * z_of(j)
+        rhs = jnp.concatenate(
+            [
+                jnp.concatenate([weights[b + s, half, group], weights[b + s, half, group + 1]], axis=1)
+                for s in range(2)
+            ],
+            axis=0,
+        )
+        return jnp.dot(hidden[j], rhs, preferred_element_type=jnp.float32)
+
+    def second_layer(first, last):
+        def body(i, carry):
+            j, n = first + lax.div(i, 8), lax.rem(i, 8)
+            if first == 0:
+                total[n] = product(j, n)
+            else:
+                total[n] += product(j, n)
+            return carry
+
+        lax.fori_loop(0, 8 * (last - first), body, 0)
+
+    near1 = [(1, 0, -1), (1, 0, 1)]
+    units(near1)
+    assemble(own_slabs, own_image)
+    relay(6)
+    relay(7)
+    for j in range(2, STEPS):
+        in_start(j)
+    quarters([twin_key])
+    in_pass(0)
+    in_pass(1)
+    own_layer(0, 3)
+    opposites([twin_key])
+    quarters(near1)
+    own_layer(3, 5)
+    opposites(near1)
+    in_pass_next(0)
+    in_pass_next(1)
+    far1 = [(1, 1, -1), (1, 1, 1)]
+    units(far1)
+    own_layer(5, 8)
+    for last in lasts:
+        last.wait_recv()
+    quarters(far1)
+    assemble(far_slabs, far_image)
+    in_complete(0)
+    in_complete(1)
+    opposites(far1)
+    in_pass(2)
+    first_layer(0, 1)
+    for (near, group), copy in own_weights.items():
+        if not near or group >= 5:
+            copy.wait()
+    complete([twin_key])
+    second_layer(0, 1)
+
+    near2 = [(2, 0, -1), (2, 0, 1)]
+    units(near2)
+    in_pass_next(2)
+    in_pass(3)
+    first_layer(1, 2)
+    quarters(near2)
+    in_pass_next(3)
+    in_complete(2)
+    first_layer(2, 3)
+    opposites(near2)
+    in_pass(4)
+    complete(near1)
+    complete(far1)
+    second_layer(1, 3)
+
+    far2 = [(2, 1, -1), (2, 1, 1)]
+    units(far2)
+    in_pass_next(4)
+    in_pass(5)
+    in_complete(3)
+    first_layer(3, 4)
+    quarters(far2)
+    in_pass_next(5)
+    in_complete(4)
+    first_layer(4, 5)
+    opposites(far2)
+    in_pass(6)
+
+    near3 = [(3, 0, -1), (3, 0, 1)]
+    units(near3)
+    complete(near2)
+    complete(far2)
+    second_layer(3, 5)
+    in_pass_next(6)
+    in_pass(7)
+    quarters(near3)
+    in_complete(5)
+    first_layer(5, 6)
+    in_pass_next(7)
+    in_complete(6)
+    opposites(near3)
+    first_layer(6, 7)
+    in_complete(7)
+    first_layer(7, 8)
+
+    far3 = [(3, 1, -1), (3, 1, 1)]
+    units(far3)
+    quarters(far3)
+    opposites(far3)
+    complete(near3)
+    complete(far3)
+    second_layer(5, 7)
+
+    final = [(4, 0, -1), (4, 1, 1)]
+    units(final)
+    quarters(final)
+    opposites(final)
+    complete(final)
+
+    def finish(n, carry):
+        half, group = lax.div(n, 4), 2 * lax.rem(n, 4)
+        value = total[n] + product(7, n)
+        for side in range(2):
+            g = group + side
+            turned = lax.rem(x + g, 4)
+            in_first = lax.div(4 + 3 - g, 4)
+            place_at = in_first * g + (1 - in_first) * (4 + turned)
+            start = pl.multiple_of(1024 * half + GROUP * place_at, GROUP)
+            part = value[:, side * GROUP : (side + 1) * GROUP] + b_out[:, pl.ds(start, GROUP)]
+            out_ref[:, pl.ds(start, GROUP)] = part.astype(jnp.bfloat16)
+        return carry
+
+    lax.fori_loop(0, 8, finish, 0)
+    for copy in sent:
+        copy.wait_send()
+
+
+LOCALS = 25
+SENDS = 160
+
+
+def project(shift, features, w_in, b_in, w_out, b_out):
+    slabs, height, width = features.shape
+    tokens = slabs * height
+    padded = tokens + TILE
+    hidden = w_in.shape[1]
+    columns = w_out.shape[1]
+    block = w_out.shape[0]
+    chunk = hidden // STEPS
+    bf16, f32 = jnp.bfloat16, jnp.float32
+    anywhere = pl.BlockSpec(memory_space=pl.ANY)
+    vmem = pl.BlockSpec(memory_space=pltpu.VMEM)
+    quarter = width // 4
+    flops = 2 * padded * (2 * width * hidden + hidden * columns)
+    return pl.pallas_call(
+        project_kernel,
+        out_shape=jax.ShapeDtypeStruct((padded, columns), bf16),
+        in_specs=[pl.BlockSpec(memory_space=pltpu.SMEM), anywhere, anywhere, vmem, anywhere, vmem],
+        out_specs=vmem,
+        scratch_shapes=[
+            pltpu.VMEM((slabs, height, width), bf16),
+            pltpu.VMEM((slabs, height, width), bf16),
+            pltpu.VMEM((slabs, height, width), bf16),
+            pltpu.VMEM((tokens, width), f32),
+            pltpu.VMEM((padded, width), bf16),
+            pltpu.VMEM((padded, width), bf16),
+            pltpu.VMEM((STEPS, 4, quarter, chunk), bf16),
+            pltpu.VMEM((STEPS, 4, quarter, chunk), bf16),
+            pltpu.VMEM((STEPS, padded, chunk), f32),
+            pltpu.VMEM((STEPS, padded, chunk), bf16),
+            pltpu.VMEM((16, 2, 8, block, GROUP), bf16),
+            pltpu.VMEM((8, padded, 2 * GROUP), f32),
+            pltpu.SemaphoreType.DMA((LOCALS,)),
+            pltpu.SemaphoreType.DMA((SENDS,)),
+            pltpu.SemaphoreType.DMA((SENDS,)),
+        ],
+        compiler_params=pltpu.CompilerParams(
+            collective_id=0, has_side_effects=True, vmem_limit_bytes=67_043_328
+        ),
+        cost_estimate=pl.CostEstimate(flops=flops, bytes_accessed=10_000_000, transcendentals=padded * hidden),
+        name="project",
+    )(shift, features, w_in.reshape(4, quarter, hidden), b_in.reshape(STEPS, chunk), w_out, b_out.reshape(1, columns))
+
+
 def on_device(features, w_in, b_in, w_out, b_out, text, offsets):
-    col = lax.axis_index("col")
-    cols = lax.axis_size("col")
-    image = lax.all_to_all(features, "col", split_axis=0, concat_axis=1, tiled=True)[0]
-    image = lax.all_gather(image, "depth", axis=1, tiled=True)
-    patch_count = image.shape[0]
-    shift = lax.rem(offsets[0], TILE)
-    spots = jnp.arange(patch_count + TILE, dtype=jnp.int32)[:, None] - shift
-    moved = (spots == jnp.arange(patch_count, dtype=jnp.int32)[None, :]).astype(jnp.bfloat16)
-    image = jnp.dot(moved, image, preferred_element_type=jnp.float32).astype(jnp.bfloat16)
-
-    part = w_in.shape[0] // cols
-    own_in = lax.dynamic_slice_in_dim(w_in, col * part, part, 0)
-    full_in = lax.all_gather(own_in, ("depth", "col"), axis=0, tiled=True)
-    pre = jnp.dot(image, full_in, preferred_element_type=jnp.float32) + b_in
-    hidden = jax.nn.gelu(pre, approximate=False).astype(jnp.bfloat16)
-
-    part = w_out.shape[0] // cols
-    own_out = lax.dynamic_slice_in_dim(w_out, col * part, part, 0)
-    full_out = lax.all_gather(own_out, ("row", "col"), axis=0, tiled=True)
-    total = jnp.dot(hidden, full_out, preferred_element_type=jnp.float32)
-    projected = (total + b_out).astype(jnp.bfloat16)
+    shift = lax.rem(offsets, TILE)
+    projected = project(shift, features, w_in, b_in, w_out, b_out)
     return place(projected, text[0], offsets)[None]
 
 

time: 400 us -> 125 us (0.31)
  waiting for transfers between devices: 310 us -> 0 us
  Pallas kernels: 4.75 us -> 123 us
  matrix products: 48.4 us -> 0 us
  blocking collectives: 18.4 us -> 0 us
  between operations: 13.8 us -> 0.67 us
    all_gather x3 -> x0, waiting for transfers between devices: 310 us -> none  [the longest x1 198 us: on_device(): full_out = lax.all_gather(own_out, ('row', 'col'), axis=0, tiled=True)]
    pallas_call x0 -> x1, Pallas kernels: none -> 118 us  [project(): pl.pallas_call(project_kernel, out_shape=jax.ShapeDtypeStruct((padded, co...]
    dot_general x3 -> x0, matrix products: 48.4 us -> none  [the longest x1 29.5 us: on_device(): pre = jnp.dot(image, full_in, preferred_element_type=jnp.float32) + b_in]
    all_to_all x1 -> x0, blocking collectives: 18.4 us -> none  [on_device(): lax.all_to_all(features, 'col', split_axis=0, concat_axis=1, tiled=True)[0]]
  transfers between devices with their start and end apart: 3 -> 0, of which waited for: 3 -> 0; matrix products, arithmetic and copies ran while one was open for 9% -> 0% of each run, Pallas kernels for 0% -> 0%
where the time goes in v2:
time: 125 us
  Pallas kernels  123 us (98%)
  local copies, waits for them, and re-layouts  1.33 us (1%)
    pallas_call x1, Pallas kernels, project(): pl.pallas_call(project_kernel, out_shape=jax.ShapeDtypeStruct((padded, co...  118 us
    pallas_call x1, Pallas kernels, place(): pl.pallas_call(place_kernel, out_shape=jax.ShapeDtypeStruct((length, colu...  4.77 us

profile of v2, /device:TPU:1, one launch (start us, length us, event | category | flops | bytes accessed | tf_op | source)
XLA Modules:
  0.0 125.0 jit_solution(14672193237735296524)
XLA Ops:
  0.7 1.3 %reshape.12.b_in = f32[8,512]{1,0:T(8,128)} reshape(f32[4096]{0:T(1024)} %param.9) | data formatting | bytes 32768 | tf_op jit(solution)/shard_map/reshape | solution.py:466
  2.0 118.2 %project.1.image_ref = bf16[592,2048]{1,0:T(8,128)(2,1)} custom-call(s32[1]{0:T(128)S(6)} %rem.18.shift_ref, bf16[8,72,576]{2,1,0:T(8,128)(2,1)} %features.1, bf16[4,144,4096]{2,1,0:T(8,128)(2,1)} %bitcast.5, f32[8,512]{1,0:T(8,128)} %reshape.12.b_in, bf16[256,2048]{1,0:T(8,128)(2,1)} %w_out.1, f32[1,2048]{1,0:T(1,128)} %bitcast.6), custom_call_target="tpu_custom_call" | custom-call | flops 15518924800 | bytes 10000000 | tf_op jit(solution)/shard_map/project/pallas_call | solution.py:439
  120.2 4.8 %place.1 = bf16[1024,2048]{1,0:T(8,128)(2,1)} custom-call(s32[1]{0:T(128)S(6)} %copy.8.offset_ref, bf16[592,2048]{1,0:T(8,128)(2,1)} %project.1.image_ref, bf16[448,2048]{1,0:T(8,128)(2,1)} %bitcast.4), custom_call_target="tpu_custom_call" | custom-call | tf_op jit(solution)/shard_map/place/pallas_call | solution.py:42

commit v3 on v2

--- a/solution.py
+++ b/solution.py
@@ -124,47 +124,61 @@
         pl.semaphore_signal(barrier, inc=1, device_id=partner, device_id_type=MESH)
     pl.semaphore_wait(barrier, len(partners))
 
-    ring_up, ring_down, unit_mate, quarter, opposite, rest_mate = {}, {}, {}, {}, {}, {}
-
-    def unit(b):
-        return weights.at[b, core, pl.ds(0, 5)]
-
-    def arrived_from(t, s, sign):
+    ring, quarter, opposite, first_mate, second_mate = {}, {}, {}, {}, {}
+
+    def columns_of(b, part):
+        return weights.at[b, core, pl.ds(0, 4)] if part == "first" else weights.at[b, core, 4]
+
+    def block_of(key):
+        t, s, sign = key
         return 2 * lax.rem(z + 8 + sign * t, 8) + (low if s == 0 else 1 - low)
 
-    def onward(b, t, s, sign):
-        ring = ring_up if sign < 0 else ring_down
+    def onward(key, part):
+        t, s, sign = key
         if t < 3 or (t == 3 and s == (0 if sign < 0 else 1)):
-            ring[t, s] = send(unit(b), unit(b), up if sign < 0 else down)
-
-    def spread(b, key):
+            b = block_of(key)
+            ring[key, part] = send(columns_of(b, part), columns_of(b, part), up if sign < 0 else down)
+
+    def came(key, part):
+        t, s, sign = key
+        ring[(t - 1, s, sign), part].wait_recv()
+
+    def spread(key):
+        b = block_of(key)
         quarter[key] = (
             send(weights.at[b, core, 4], weights.at[b, core, 7], ahead),
             send(weights.at[b, core, 4], weights.at[b, core, 5], behind),
         )
-        unit_mate[key] = send(unit(b), unit(b), mate)
-
-    def block_of(key):
-        t, s, sign = key
-        return arrived_from(t, s, sign)
-
-    def units(keys):
-        for key in keys:
-            t, s, sign = key
-            (ring_up if sign < 0 else ring_down)[t - 1, s].wait_recv()
-            onward(block_of(key), t, s, sign)
-        for key in keys:
-            spread(block_of(key), key)
+
+    def pass_first(key):
+        b = block_of(key)
+        first_mate[key] = send(columns_of(b, "first"), columns_of(b, "first"), mate)
+
+    def firsts(keys):
+        for key in keys:
+            came(key, "first")
+            onward(key, "first")
+        for key in keys:
+            pass_first(key)
+
+    def seconds(keys):
+        for key in keys:
+            came(key, "second")
+            onward(key, "second")
+
+    def spreads(keys):
+        for key in keys:
+            spread(key)
 
     def quarters(keys):
         for key in keys:
             b = block_of(key)
             for copy in quarter[key]:
                 copy.wait_recv()
-            first, second = pl.ds(0, 128), pl.ds(128, 128)
+            above, below = pl.ds(0, 128), pl.ds(128, 128)
             opposite[key] = (
-                send(weights.at[b, core, 7, first], weights.at[b, core, 6, first], ahead),
-                send(weights.at[b, core, 5, second], weights.at[b, core, 6, second], behind),
+                send(weights.at[b, core, 7, above], weights.at[b, core, 6, above], ahead),
+                send(weights.at[b, core, 5, below], weights.at[b, core, 6, below], behind),
             )
 
     def opposites(keys):
@@ -172,18 +186,33 @@
             b = block_of(key)
             for copy in opposite[key]:
                 copy.wait_recv()
-            rest_mate[key] = send(weights.at[b, core, pl.ds(5, 3)], weights.at[b, core, pl.ds(5, 3)], mate)
+            second_mate[key] = send(weights.at[b, core, pl.ds(4, 4)], weights.at[b, core, pl.ds(4, 4)], mate)
 
     def complete(keys):
         for key in keys:
-            unit_mate[key].wait_recv()
-            rest_mate[key].wait_recv()
-
-    for group in range(5):
+            first_mate[key].wait_recv()
+            second_mate[key].wait_recv()
+
+    def twin_seconds():
+        twin_second.wait_recv()
+        onward((0, 1, -1), "second")
+        onward((0, 1, 1), "second")
+
+    def twin_firsts():
+        twin_first.wait_recv()
+        onward((0, 1, -1), "first")
+        onward((0, 1, 1), "first")
+        pass_first((0, 1, 1))
+
+    own_weights[True, 4].wait()
+    onward((0, 0, -1), "second")
+    onward((0, 0, 1), "second")
+    twin_second = send(columns_of(row, "second"), columns_of(row, "second"), beside)
+    for group in range(4):
         own_weights[True, group].wait()
-    onward(row, 0, 0, -1)
-    onward(row, 0, 0, 1)
-    twin_unit = send(unit(row), unit(row), beside)
+    onward((0, 0, -1), "first")
+    onward((0, 0, 1), "first")
+    twin_first = send(columns_of(row, "first"), columns_of(row, "first"), beside)
     slab_copies = {}
     for other in [others[1], others[2], others[3], others[4], others[5], others[6], others[0]]:
         target = column(*other)
@@ -209,44 +238,29 @@
         in_mate[j].wait_recv()
         in_mate_next[j].wait_recv()
 
-    in_start(0)
-    in_start(1)
-
-    hops, lasts, slab_at = [], [], []
-
-    def hop(slab):
-        n = len(hops)
-        slab_at.append(slab)
-        hops.append(send(own_slabs.at[slab], relay_slabs.at[slab], beside if n % 2 == 0 else across))
+
+    hops, lasts, slab_at = {}, {}, {}
+
+    def hop(n, slab):
+        slab_at[n] = slab
+        hops[n] = send(own_slabs.at[slab], relay_slabs.at[slab], beside if n % 2 == 0 else across)
 
     def relay(n):
         hops[n].wait_recv()
         slab = slab_at[n]
-        lasts.append(send(relay_slabs.at[slab], far_slabs.at[slab], across if n % 2 == 0 else beside))
+        lasts[n] = send(relay_slabs.at[slab], far_slabs.at[slab], across if n % 2 == 0 else beside)
 
     def source_of(other):
         step, flip = other
         return column((4 - step) % 4, flip)
 
-    def take(other):
-        slab_copies[other].wait_recv()
-        hop(source_of(other))
-
-    own_slab.wait()
-    hop(col)
-    for other in (others[0], others[1], others[2], others[3], others[4]):
-        take(other)
-    relay(0)
-    relay(1)
-    twin_unit.wait_recv()
-    twin_key = (0, 1, 1)
-    onward(twin, 0, 1, -1)
-    onward(twin, 0, 1, 1)
-    spread(twin, twin_key)
-    take(others[5])
-    take(others[6])
-    for n in range(2, 6):
-        relay(n)
+    def take(n):
+        if n == 0:
+            own_slab.wait()
+            hop(0, col)
+        else:
+            slab_copies[others[n - 1]].wait_recv()
+            hop(n, source_of(others[n - 1]))
 
     patch_count = tokens.shape[0]
     spots = lax.broadcasted_iota(jnp.int32, (patch_count + TILE, patch_count), 0) - shift_ref[0]
@@ -277,15 +291,14 @@
             j, n = lax.div(i, 2), lax.rem(i, 2)
             rhs = far_in[j, :, :, half_columns(n)].reshape(-1, 256)
             value = pre[j, :, half_columns(n)] + jnp.dot(far_image[...], rhs, preferred_element_type=jnp.float32)
-            value = value + b_in[pl.ds(z_of(j), 1), half_columns(n)]
+            value = value + b_in[:, pl.ds(pl.multiple_of(512 * z_of(j) + 256 * n, 256), 256)]
             value = 0.5 * value * (1.0 + lax.erf(value * 0.7071067811865476))
             hidden[j, :, half_columns(n)] = value.astype(jnp.bfloat16)
             return carry
 
         lax.fori_loop(2 * first, 2 * last, body, 0)
 
-    def product(j, n):
-        half, group = lax.div(n, 4), 2 * lax.rem(n, 4)
+    def product(j, half, group):
         b = 2 * z_of(j)
         rhs = jnp.concatenate(
             [
@@ -298,129 +311,194 @@
 
     def second_layer(first, last):
         def body(i, carry):
-            j, n = first + lax.div(i, 8), lax.rem(i, 8)
-            if first == 0:
-                total[n] = product(j, n)
-            else:
-                total[n] += product(j, n)
+            j, half = first + lax.div(i, 2), lax.rem(i, 2)
+            for pair in range(4):
+                n = 4 * half + pair
+                if first == 0:
+                    total[n] = product(j, half, 2 * pair)
+                else:
+                    total[n] += product(j, half, 2 * pair)
             return carry
 
-        lax.fori_loop(0, 8 * (last - first), body, 0)
-
-    near1 = [(1, 0, -1), (1, 0, 1)]
-    units(near1)
+        lax.fori_loop(0, 2 * (last - first), body, 0)
+
+    in_start(0)
+    take(0)
+    in_start(1)
+    seconds([(1, 0, 1)])
+    seconds([(1, 0, -1)])
+    in_start(2)
+    in_start(3)
+    in_pass(0)
+    twin_seconds()
+    spreads([(1, 0, -1)])
+    spreads([(0, 1, 1)])
+    twin_firsts()
+    take(2)
+    seconds([(1, 1, 1)])
+    take(6)
+    take(3)
+    take(1)
+    seconds([(1, 1, -1)])
+    seconds([(2, 0, 1)])
+    spreads([(2, 0, 1)])
+    spreads([(1, 1, -1)])
+    in_pass(2)
+    quarters([(0, 1, 1)])
+    seconds([(2, 0, -1)])
+    take(7)
+    take(4)
+    take(5)
     assemble(own_slabs, own_image)
+    spreads([(1, 1, 1)])
+    firsts([(1, 0, -1)])
+    relay(3)
+    spreads([(2, 0, -1)])
+    firsts([(1, 1, 1)])
+    relay(2)
+    seconds([(2, 1, -1)])
+    spreads([(2, 1, -1)])
+    relay(0)
+    opposites([(0, 1, 1)])
+    own_layer(0, 1)
+    seconds([(2, 1, 1)])
+    spreads([(2, 1, 1)])
+    in_start(4)
+    in_pass(1)
+    firsts([(1, 0, 1)])
+    firsts([(1, 1, -1)])
+    seconds([(3, 0, 1)])
+    quarters([(2, 0, 1)])
+    relay(5)
     relay(6)
+    relay(4)
+    quarters([(1, 0, -1)])
+    quarters([(2, 0, -1)])
+    in_start(5)
+    own_layer(1, 2)
     relay(7)
-    for j in range(2, STEPS):
-        in_start(j)
-    quarters([twin_key])
-    in_pass(0)
-    in_pass(1)
-    own_layer(0, 3)
-    opposites([twin_key])
-    quarters(near1)
-    own_layer(3, 5)
-    opposites(near1)
+    relay(1)
+    seconds([(3, 0, -1)])
+    spreads([(3, 0, 1)])
+    quarters([(1, 1, 1)])
+    own_layer(2, 3)
+    in_start(6)
+    quarters([(2, 1, -1)])
+    spreads([(3, 0, -1)])
+    own_layer(3, 6)
     in_pass_next(0)
+    in_start(7)
+    quarters([(1, 1, -1)])
+    seconds([(3, 1, -1)])
+    quarters([(2, 1, 1)])
+    opposites([(2, 0, -1)])
+    in_pass_next(2)
+    opposites([(1, 0, -1)])
+    firsts([(2, 0, -1)])
+    in_pass(3)
     in_pass_next(1)
-    far1 = [(1, 1, -1), (1, 1, 1)]
-    units(far1)
-    own_layer(5, 8)
-    for last in lasts:
+    seconds([(3, 1, 1)])
+    spreads([(3, 1, -1)])
+    in_pass(4)
+    spreads([(3, 1, 1)])
+    firsts([(2, 1, 1)])
+    spreads([(1, 0, 1)])
+    own_layer(6, 7)
+    opposites([(2, 1, -1)])
+    own_layer(7, 8)
+    for last in lasts.values():
         last.wait_recv()
-    quarters(far1)
     assemble(far_slabs, far_image)
+    opposites([(1, 1, 1)])
     in_complete(0)
-    in_complete(1)
-    opposites(far1)
-    in_pass(2)
     first_layer(0, 1)
+    firsts([(2, 0, 1)])
+    quarters([(3, 1, -1)])
+    in_complete(2)
+    first_layer(2, 3)
+    firsts([(2, 1, -1)])
+    seconds([(4, 1, 1)])
+    quarters([(3, 0, 1)])
+    in_pass_next(3)
+    spreads([(4, 1, 1)])
+    seconds([(4, 0, -1)])
+    in_pass(5)
     for (near, group), copy in own_weights.items():
         if not near or group >= 5:
             copy.wait()
-    complete([twin_key])
+    complete([(0, 1, 1)])
     second_layer(0, 1)
-
-    near2 = [(2, 0, -1), (2, 0, 1)]
-    units(near2)
-    in_pass_next(2)
-    in_pass(3)
+    quarters([(3, 1, 1)])
+    spreads([(4, 0, -1)])
+    in_complete(1)
     first_layer(1, 2)
-    quarters(near2)
-    in_pass_next(3)
-    in_complete(2)
-    first_layer(2, 3)
-    opposites(near2)
-    in_pass(4)
-    complete(near1)
-    complete(far1)
-    second_layer(1, 3)
-
-    far2 = [(2, 1, -1), (2, 1, 1)]
-    units(far2)
+    quarters([(1, 0, 1)])
+    in_pass(6)
+    opposites([(1, 1, -1)])
     in_pass_next(4)
-    in_pass(5)
+    quarters([(3, 0, -1)])
+    opposites([(2, 1, 1)])
     in_complete(3)
     first_layer(3, 4)
-    quarters(far2)
-    in_pass_next(5)
+    opposites([(2, 0, 1)])
+    complete([(2, 0, -1), (2, 1, -1)])
+    second_layer(3, 4)
     in_complete(4)
     first_layer(4, 5)
-    opposites(far2)
-    in_pass(6)
-
-    near3 = [(3, 0, -1), (3, 0, 1)]
-    units(near3)
-    complete(near2)
-    complete(far2)
-    second_layer(3, 5)
-    in_pass_next(6)
+    in_pass_next(5)
+    firsts([(3, 1, 1)])
+    firsts([(3, 0, -1)])
+    opposites([(3, 1, -1)])
+    quarters([(4, 1, 1)])
     in_pass(7)
-    quarters(near3)
+    complete([(2, 0, 1), (2, 1, 1)])
+    second_layer(4, 5)
+    opposites([(3, 1, 1)])
     in_complete(5)
     first_layer(5, 6)
+    in_pass_next(6)
+    opposites([(3, 0, 1)])
+    quarters([(4, 0, -1)])
+    firsts([(3, 0, 1)])
+    opposites([(3, 0, -1)])
+    opposites([(1, 0, 1)])
+    complete([(1, 0, -1), (1, 1, -1)])
+    second_layer(1, 2)
+    firsts([(3, 1, -1)])
+    in_complete(6)
+    first_layer(6, 7)
+    complete([(3, 0, 1), (3, 1, 1)])
+    second_layer(6, 7)
+    opposites([(4, 0, -1)])
     in_pass_next(7)
-    in_complete(6)
-    opposites(near3)
-    first_layer(6, 7)
+    opposites([(4, 1, 1)])
+    complete([(3, 0, -1), (3, 1, -1)])
+    second_layer(5, 6)
+    firsts([(4, 1, 1)])
+    firsts([(4, 0, -1)])
+    complete([(1, 0, 1), (1, 1, 1)])
+    second_layer(2, 3)
     in_complete(7)
     first_layer(7, 8)
-
-    far3 = [(3, 1, -1), (3, 1, 1)]
-    units(far3)
-    quarters(far3)
-    opposites(far3)
-    complete(near3)
-    complete(far3)
-    second_layer(5, 7)
-
-    final = [(4, 0, -1), (4, 1, 1)]
-    units(final)
-    quarters(final)
-    opposites(final)
-    complete(final)
-
-    def finish(n, carry):
-        half, group = lax.div(n, 4), 2 * lax.rem(n, 4)
-        value = total[n] + product(7, n)
-        for side in range(2):
-            g = group + side
-            turned = lax.rem(x + g, 4)
-            in_first = lax.div(4 + 3 - g, 4)
-            place_at = in_first * g + (1 - in_first) * (4 + turned)
-            start = pl.multiple_of(1024 * half + GROUP * place_at, GROUP)
-            part = value[:, side * GROUP : (side + 1) * GROUP] + b_out[:, pl.ds(start, GROUP)]
-            out_ref[:, pl.ds(start, GROUP)] = part.astype(jnp.bfloat16)
+    complete([(4, 0, -1), (4, 1, 1)])
+
+    def finish(half, carry):
+        for pair in range(4):
+            value = total[4 * half + pair] + product(7, half, 2 * pair)
+            for side in range(2):
+                group = 2 * pair + side
+                start = pl.multiple_of(group_column(half, group), GROUP)
+                part = value[:, side * GROUP : (side + 1) * GROUP] + b_out[:, pl.ds(start, GROUP)]
+                out_ref[:, pl.ds(start, GROUP)] = part.astype(jnp.bfloat16)
         return carry
 
-    lax.fori_loop(0, 8, finish, 0)
+    lax.fori_loop(0, 2, finish, 0)
     for copy in sent:
         copy.wait_send()
 
 
 LOCALS = 25
-SENDS = 160
+SENDS = 175
 
 
 def project(shift, features, w_in, b_in, w_out, b_out):
@@ -432,7 +510,7 @@
     block = w_out.shape[0]
     chunk = hidden // STEPS
     bf16, f32 = jnp.bfloat16, jnp.float32
-    anywhere = pl.BlockSpec(memory_space=pl.ANY)
+    anywhere = pl.BlockSpec(memory_space=pltpu.HBM)
     vmem = pl.BlockSpec(memory_space=pltpu.VMEM)
     quarter = width // 4
     flops = 2 * padded * (2 * width * hidden + hidden * columns)
@@ -459,11 +537,11 @@
             pltpu.SemaphoreType.DMA((SENDS,)),
         ],
         compiler_params=pltpu.CompilerParams(
-            collective_id=0, has_side_effects=True, vmem_limit_bytes=67_043_328
+            collective_id=0, has_side_effects=True, vmem_limit_bytes=58_000_000
         ),
         cost_estimate=pl.CostEstimate(flops=flops, bytes_accessed=10_000_000, transcendentals=padded * hidden),
         name="project",
-    )(shift, features, w_in.reshape(4, quarter, hidden), b_in.reshape(STEPS, chunk), w_out, b_out.reshape(1, columns))
+    )(shift, features, w_in.reshape(4, quarter, hidden), b_in.reshape(1, hidden), w_out, b_out.reshape(1, columns))
 
 
 def on_device(features, w_in, b_in, w_out, b_out, text, offsets):

time: 125 us -> 77.6 us (0.62)
  Pallas kernels: 123 us -> 76.7 us
  local copies, waits for them, and re-layouts: 1.33 us -> 0 us
    pallas_call x1, Pallas kernels: 118 us -> 71.9 us  [project(): pl.pallas_call(project_kernel, out_shape=jax.ShapeDtypeStruct((padded, co...]
    reshape x1 -> x0, local copies, waits for them, and re-layouts: 1.33 us -> none  [project(): b_in.reshape(STEPS, chunk)]
where the time goes in v3:
time: 77.6 us; the launch traced here: 77.3 us
  Pallas kernels  76.7 us (99%)
    pallas_call x1, Pallas kernels, project(): pl.pallas_call(project_kernel, out_shape=jax.ShapeDtypeStruct((padded, co...  71.9 us
    pallas_call x1, Pallas kernels, place(): pl.pallas_call(place_kernel, out_shape=jax.ShapeDtypeStruct((length, colu...  4.77 us

profile of v3, /device:TPU:1, one launch (start us, length us, event | category | flops | bytes accessed | tf_op | source)
XLA Modules:
  0.0 77.3 jit_solution(13721670660127178095)
XLA Ops:
  0.7 71.9 %project.1.image_ref = bf16[592,2048]{1,0:T(8,128)(2,1)} custom-call(s32[1]{0:T(128)S(6)} %rem.18.shift_ref, bf16[8,72,576]{2,1,0:T(8,128)(2,1)} %features.1, bf16[4,144,4096]{2,1,0:T(8,128)(2,1)} %bitcast.6, f32[1,4096]{1,0:T(1,128)} %bitcast.7, bf16[256,2048]{1,0:T(8,128)(2,1)} %w_out.1, f32[1,2048]{1,0:T(1,128)} %bitcast.8), custom_call_target="tpu_custom_call" | custom-call | flops 15518924800 | bytes 10000000 | tf_op jit(solution)/shard_map/project/pallas_call | solution.py:517
  72.6 4.8 %place.1 = bf16[1024,2048]{1,0:T(8,128)(2,1)} custom-call(s32[1]{0:T(128)S(6)} %copy.8.offset_ref, bf16[592,2048]{1,0:T(8,128)(2,1)} %project.1.image_ref, bf16[448,2048]{1,0:T(8,128)(2,1)} %bitcast.5), custom_call_target="tpu_custom_call" | custom-call | tf_op jit(solution)/shard_map/place/pallas_call | solution.py:42

commit v4 on v3

--- a/solution.py
+++ b/solution.py
@@ -35,7 +35,7 @@
         out_ref[pl.ds(pl.multiple_of(base + patch_count, TILE), TILE), :] = below
 
 
-def place(image_rows, text_rows, offset, width=512):
+def place(image_rows, text_rows, offset, width=1024):
     padded, columns = image_rows.shape
     text_count = text_rows.shape[0]
     length = padded - TILE + text_count
@@ -58,7 +58,7 @@
 def project_kernel(
     shift_ref, features, w_in, b_in, w_out, b_out, out_ref,
     own_slabs, relay_slabs, far_slabs, tokens, own_image, far_image,
-    own_in, far_in, pre, hidden, weights, total,
+    own_in, far_in, pre, hidden, weights, total, out_rows,
     local_sem, send_sem, recv_sem,
 ):
     depth, row, col = lax.axis_index("depth"), lax.axis_index("row"), lax.axis_index("col")
@@ -274,29 +274,18 @@
             moved, tokens[...].astype(jnp.bfloat16), preferred_element_type=jnp.float32
         ).astype(jnp.bfloat16)
 
-    def half_columns(n):
-        return pl.ds(pl.multiple_of(256 * n, 256), 256)
-
     def own_layer(first, last):
-        def body(i, carry):
-            j, n = lax.div(i, 2), lax.rem(i, 2)
-            rhs = own_in[j, :, :, half_columns(n)].reshape(-1, 256)
-            pre[j, :, half_columns(n)] = jnp.dot(own_image[...], rhs, preferred_element_type=jnp.float32)
-            return carry
-
-        lax.fori_loop(2 * first, 2 * last, body, 0)
+        for j in range(first, last):
+            pre[j] = jnp.dot(own_image[...], own_in[j].reshape(-1, 512), preferred_element_type=jnp.float32)
 
     def first_layer(first, last):
-        def body(i, carry):
-            j, n = lax.div(i, 2), lax.rem(i, 2)
-            rhs = far_in[j, :, :, half_columns(n)].reshape(-1, 256)
-            value = pre[j, :, half_columns(n)] + jnp.dot(far_image[...], rhs, preferred_element_type=jnp.float32)
-            value = value + b_in[:, pl.ds(pl.multiple_of(512 * z_of(j) + 256 * n, 256), 256)]
+        for j in range(first, last):
+            value = pre[j] + jnp.dot(
+                far_image[...], far_in[j].reshape(-1, 512), preferred_element_type=jnp.float32
+            )
+            value = value + b_in[:, pl.ds(pl.multiple_of(512 * z_of(j), 512), 512)]
             value = 0.5 * value * (1.0 + lax.erf(value * 0.7071067811865476))
-            hidden[j, :, half_columns(n)] = value.astype(jnp.bfloat16)
-            return carry
-
-        lax.fori_loop(2 * first, 2 * last, body, 0)
+            hidden[j] = value.astype(jnp.bfloat16)
 
     def product(j, half, group):
         b = 2 * z_of(j)
@@ -310,17 +299,14 @@
         return jnp.dot(hidden[j], rhs, preferred_element_type=jnp.float32)
 
     def second_layer(first, last):
-        def body(i, carry):
-            j, half = first + lax.div(i, 2), lax.rem(i, 2)
-            for pair in range(4):
-                n = 4 * half + pair
-                if first == 0:
-                    total[n] = product(j, half, 2 * pair)
-                else:
-                    total[n] += product(j, half, 2 * pair)
-            return carry
-
-        lax.fori_loop(0, 2 * (last - first), body, 0)
+        for j in range(first, last):
+            for half in range(2):
+                for pair in range(4):
+                    n = 4 * half + pair
+                    if j == 0:
+                        total[n] = product(j, half, 2 * pair)
+                    else:
+                        total[n] += product(j, half, 2 * pair)
 
     in_start(0)
     take(0)
@@ -482,22 +468,27 @@
     first_layer(7, 8)
     complete([(4, 0, -1), (4, 1, 1)])
 
-    def finish(half, carry):
+    def finish(half):
         for pair in range(4):
             value = total[4 * half + pair] + product(7, half, 2 * pair)
             for side in range(2):
                 group = 2 * pair + side
                 start = pl.multiple_of(group_column(half, group), GROUP)
                 part = value[:, side * GROUP : (side + 1) * GROUP] + b_out[:, pl.ds(start, GROUP)]
-                out_ref[:, pl.ds(start, GROUP)] = part.astype(jnp.bfloat16)
-        return carry
-
-    lax.fori_loop(0, 2, finish, 0)
+                out_rows[:, pl.ds(start, GROUP)] = part.astype(jnp.bfloat16)
+
+    outs = []
+    for half in range(2):
+        finish(half)
+        columns = pl.ds(1024 * half, 1024)
+        outs.append(local(out_rows.at[:, columns], out_ref.at[:, columns]))
+    for copy in outs:
+        copy.wait()
     for copy in sent:
         copy.wait_send()
 
 
-LOCALS = 25
+LOCALS = 27
 SENDS = 175
 
 
@@ -518,7 +509,7 @@
         project_kernel,
         out_shape=jax.ShapeDtypeStruct((padded, columns), bf16),
         in_specs=[pl.BlockSpec(memory_space=pltpu.SMEM), anywhere, anywhere, vmem, anywhere, vmem],
-        out_specs=vmem,
+        out_specs=anywhere,
         scratch_shapes=[
             pltpu.VMEM((slabs, height, width), bf16),
             pltpu.VMEM((slabs, height, width), bf16),
@@ -532,12 +523,13 @@
             pltpu.VMEM((STEPS, padded, chunk), bf16),
             pltpu.VMEM((16, 2, 8, block, GROUP), bf16),
             pltpu.VMEM((8, padded, 2 * GROUP), f32),
+            pltpu.VMEM((padded, columns), bf16),
             pltpu.SemaphoreType.DMA((LOCALS,)),
             pltpu.SemaphoreType.DMA((SENDS,)),
             pltpu.SemaphoreType.DMA((SENDS,)),
         ],
         compiler_params=pltpu.CompilerParams(
-            collective_id=0, has_side_effects=True, vmem_limit_bytes=58_000_000
+            collective_id=0, has_side_effects=True, vmem_limit_bytes=67_043_328
         ),
         cost_estimate=pl.CostEstimate(flops=flops, bytes_accessed=10_000_000, transcendentals=padded * hidden),
         name="project",

time: 77.6 us -> 75.7 us (0.976)
  Pallas kernels: 76.7 us -> 74.8 us
    pallas_call x1, Pallas kernels: 4.77 us -> 3.77 us  [place(): pl.pallas_call(place_kernel, out_shape=jax.ShapeDtypeStruct((length, colu...]
    pallas_call x1, Pallas kernels: 71.9 us -> 71.1 us  [project(): pl.pallas_call(project_kernel, out_shape=jax.ShapeDtypeStruct((padded, co...]
where the time goes in v4:
time: 75.7 us; the launch traced here: 75.5 us
  Pallas kernels  74.8 us (99%)
    pallas_call x1, Pallas kernels, project(): pl.pallas_call(project_kernel, out_shape=jax.ShapeDtypeStruct((padded, co...  71.1 us
    pallas_call x1, Pallas kernels, place(): pl.pallas_call(place_kernel, out_shape=jax.ShapeDtypeStruct((length, colu...  3.77 us

profile of v4, /device:TPU:1, one launch (start us, length us, event | category | flops | bytes accessed | tf_op | source)
XLA Modules:
  0.0 75.5 jit_solution(3006756595049412506)
XLA Ops:
  0.7 71.1 %project.1.image_ref = bf16[592,2048]{1,0:T(8,128)(2,1)} custom-call(s32[1]{0:T(128)S(6)} %rem.18.shift_ref, bf16[8,72,576]{2,1,0:T(8,128)(2,1)} %features.1, bf16[4,144,4096]{2,1,0:T(8,128)(2,1)} %bitcast.6, f32[1,4096]{1,0:T(1,128)} %bitcast.7, bf16[256,2048]{1,0:T(8,128)(2,1)} %w_out.1, f32[1,2048]{1,0:T(1,128)} %bitcast.8), custom_call_target="tpu_custom_call" | custom-call | flops 15518924800 | bytes 10000000 | tf_op jit(solution)/shard_map/project/pallas_call | solution.py:508
  71.8 3.8 %place.1 = bf16[1024,2048]{1,0:T(8,128)(2,1)} custom-call(s32[1]{0:T(128)S(6)} %copy.8.offset_ref, bf16[592,2048]{1,0:T(8,128)(2,1)} %project.1.image_ref, bf16[448,2048]{1,0:T(8,128)(2,1)} %bitcast.5), custom_call_target="tpu_custom_call" | custom-call | tf_op jit(solution)/shard_map/place/pallas_call | solution.py:42

commit v5 on v4

--- a/solution.py
+++ b/solution.py
@@ -466,7 +466,6 @@
     second_layer(2, 3)
     in_complete(7)
     first_layer(7, 8)
-    complete([(4, 0, -1), (4, 1, 1)])
 
     def finish(half):
         for pair in range(4):
@@ -478,9 +477,11 @@
                 out_rows[:, pl.ds(start, GROUP)] = part.astype(jnp.bfloat16)
 
     outs = []
-    for half in range(2):
+    for half in (core, 1 - core):
+        if half is not core:
+            complete([(4, 0, -1), (4, 1, 1)])
         finish(half)
-        columns = pl.ds(1024 * half, 1024)
+        columns = pl.ds(pl.multiple_of(1024 * half, 1024), 1024)
         outs.append(local(out_rows.at[:, columns], out_ref.at[:, columns]))
     for copy in outs:
         copy.wait()

time: 75.7 us -> 75.2 us (level)
  no operation moved by 1% of the time
where the time goes in v5:
time: 75.2 us; the launch traced here: 74.9 us
  Pallas kernels  74.3 us (99%)
    pallas_call x1, Pallas kernels, project(): pl.pallas_call(project_kernel, out_shape=jax.ShapeDtypeStruct((padded, co...  70.5 us
    pallas_call x1, Pallas kernels, place(): pl.pallas_call(place_kernel, out_shape=jax.ShapeDtypeStruct((length, colu...  3.77 us

profile of v5, /device:TPU:1, one launch (start us, length us, event | category | flops | bytes accessed | tf_op | source)
XLA Modules:
  0.0 74.9 jit_solution(8687111451264590232)
XLA Ops:
  0.7 70.5 %project.1.image_ref = bf16[592,2048]{1,0:T(8,128)(2,1)} custom-call(s32[1]{0:T(128)S(6)} %rem.18.shift_ref, bf16[8,72,576]{2,1,0:T(8,128)(2,1)} %features.1, bf16[4,144,4096]{2,1,0:T(8,128)(2,1)} %bitcast.6, f32[1,4096]{1,0:T(1,128)} %bitcast.7, bf16[256,2048]{1,0:T(8,128)(2,1)} %w_out.1, f32[1,2048]{1,0:T(1,128)} %bitcast.8), custom_call_target="tpu_custom_call" | custom-call | flops 15518924800 | bytes 10000000 | tf_op jit(solution)/shard_map/project/pallas_call | solution.py:509
  71.2 3.8 %place.1 = bf16[1024,2048]{1,0:T(8,128)(2,1)} custom-call(s32[1]{0:T(128)S(6)} %copy.8.offset_ref, bf16[592,2048]{1,0:T(8,128)(2,1)} %project.1.image_ref, bf16[448,2048]{1,0:T(8,128)(2,1)} %bitcast.5), custom_call_target="tpu_custom_call" | custom-call | tf_op jit(solution)/shard_map/place/pallas_call | solution.py:42
